TPU v7x, 32 devices: a whole 2x2x4 slice. The times are simulated.
32 devices in a mesh: dp: 8 (over y, x, core), tensor: 4 (over z).
Axes of the slice: x: 2, y: 2, z: 4, core: 2. Of those that a mesh axis runs over, the one named last changes fastest.
Arguments:
- tokens: bfloat16 [4096, 1536], P('dp', 'tensor'), may hold values from -6 to 6
- cotangent: bfloat16 [4096, 1536], P('dp', 'tensor'), may hold values from -6 to 6
- seq_lens: int32 [8, 3], P('dp'), may hold values from 0 to 384, as said below
- input_norm_gain: float32 [1536], replicated, may hold values from 0.5 to 1.5
- w_zx: bfloat16 [1536, 2, 3072], P(None, None, 'tensor'), may hold values from -0.15625 to 0.15625
- w_bc: bfloat16 [1536, 256], replicated, may hold values from -0.15625 to 0.15625
- w_dt: bfloat16 [1536, 48], P(None, 'tensor'), may hold values from -0.078125 to 0.078125
- conv_wx: float32 [4, 3072], P(None, 'tensor'), may hold values from -3 to 3
- conv_bx: float32 [3072], P('tensor'), may hold values from -3 to 3
- conv_wbc: float32 [4, 256], replicated, may hold values from -3 to 3
- conv_bbc: float32 [256], replicated, may hold values from -3 to 3
- a_log: float32 [48], P('tensor'), may hold values from 0 to 2.7
- dt_bias: float32 [48], P('tensor'), may hold values from -6 to -2
- d_skip: float32 [48], P('tensor'), may hold values from 0.5 to 1.5
- norm_gate: float32 [3072], P('tensor'), may hold values from 0.5 to 1.5
- w_out: bfloat16 [3072, 1536], P('tensor'), may hold values from -0.109375 to 0.109375
Outputs:
- block_out: bfloat16 [4096, 1536], P('dp', 'tensor')
- d_tokens: float32 [4096, 1536], P('dp', 'tensor')
- grad_zx: float32 [1536, 2, 3072], P('dp', None, 'tensor')
- grad_bc: float32 [1536, 256], P('dp')
- grad_dt: float32 [1536, 48], P('dp', 'tensor')
- grad_out: float32 [3072, 1536], P('tensor', 'dp')
- grad_conv_wx: float32 [4, 3072], P(None, 'tensor')
- grad_conv_bx: float32 [3072], P('tensor')
- grad_conv_wbc: float32 [4, 256], replicated
- grad_conv_bbc: float32 [256], replicated
- grad_a_log: float32 [48], P('tensor')
- grad_dt_bias: float32 [48], P('tensor')
- grad_d_skip: float32 [48], P('tensor')
- grad_gate: float32 [3072], P('tensor')
- grad_in: float32 [1536], P('tensor')
Inputs may be any that keep to these rules, and one draw needn't show every extreme that they name: `seq_lens`: row d holds the lengths of the sequences packed in order from the first row of index d of dp; the rows after them are padding. Every row has exactly one length 384, its other lengths are at most 64, it sums to at most 512, and some row sums to exactly 512.
All inputs are finite; a program needn't handle non-finite values.
Results may differ from a plain program's by a relative error of at most 0.0076.
Values may be sent and summed in bfloat16 or wider, within the bound.
A program may use at most 192 MiB of HBM per device.

v0:
```python
from functools import partial
import jax
import jax.numpy as jnp
from jax import lax
from jax.sharding import PartitionSpec as P

D = 1536
SCAN_BLOCK = 256
INNER = 3072
NORM_EPS = 1e-05
PRECISE = lax.Precision.HIGHEST


def contract_rows(first_op, second_op):
    return lax.dot_general(
        first_op, second_op, (((0,), (0,)), ((), ())), preferred_element_type=jnp.float32
    )


def contract_cols(first_op, second_op):
    return lax.dot_general(
        first_op, second_op, (((1,), (1,)), ((), ())), preferred_element_type=jnp.float32
    )


def segment_ids(lengths, row_count):
    seq_ends = jnp.cumsum(lengths)
    positions = jnp.arange(row_count, dtype=jnp.int32)
    return jnp.sum((positions[:, None] >= seq_ends[None, :]).astype(jnp.int32), axis=1)


def causal_conv(signal, kernel_w, kernel_b, segment):
    kernel_len = kernel_w.shape[0]
    row_count = signal.shape[0]
    summed = kernel_b[None, :] + kernel_w[kernel_len - 1][None, :] * signal
    for lag_steps in range(1, kernel_len):
        shifted = jnp.concatenate(
            [jnp.zeros((lag_steps, signal.shape[1]), jnp.float32), signal[: row_count - lag_steps]],
            axis=0,
        )
        earlier = jnp.concatenate(
            [jnp.full((lag_steps,), -1, jnp.int32), segment[: row_count - lag_steps]]
        )
        same_seq = (earlier == segment).astype(signal.dtype)
        summed = (
            summed + kernel_w[kernel_len - 1 - lag_steps][None, :] * shifted * same_seq[:, None]
        )
    return summed


def ssd_scan(values, steps_dt, decay_rate, b_mat, c_mat, segment, block_len):
    row_count, heads_n, head_size = values.shape
    state_n = b_mat.shape[1]
    blocks_n = row_count // block_len
    log_decay = steps_dt * decay_rate[None, :]
    seg_lasts = segment[block_len - 1 :: block_len]
    prev_lasts = jnp.concatenate([jnp.full((1,), -1, jnp.int32), seg_lasts[:-1]])
    lower_tri = jnp.arange(block_len)[:, None] >= jnp.arange(block_len)[None, :]

    def blocked(source_arr):
        return source_arr.reshape((blocks_n, block_len) + source_arr.shape[1:])

    def one_block(carry_state, block_in):
        block_vals, block_decay, block_dt, block_b, block_c, block_seg, before_seg = block_in
        cumulated = jnp.cumsum(block_decay, axis=0)
        same_seq = ((block_seg[:, None] == block_seg[None, :]) & lower_tri)[:, :, None]
        log_gaps = cumulated[:, None, :] - cumulated[None, :, :]
        decays = jnp.where(same_seq, jnp.exp(jnp.where(same_seq, log_gaps, 0.0)), 0.0)
        scores = jnp.einsum("in,jn->ij", block_c, block_b, precision=PRECISE)
        mixing = decays * scores[:, :, None] * block_dt[None, :, :]
        intra_out = jnp.einsum("ijh,jhp->ihp", mixing, block_vals, precision=PRECISE)
        keep_in = (block_seg == before_seg).astype(block_vals.dtype)
        entering = jnp.exp(cumulated) * keep_in[:, None]
        inter_out = (
            jnp.einsum("in,hnp->ihp", block_c, carry_state, precision=PRECISE)
            * entering[:, :, None]
        )
        tail_in = (block_seg == block_seg[-1]).astype(block_vals.dtype)
        to_end = jnp.exp(cumulated[-1][None, :] - cumulated) * tail_in[:, None] * block_dt
        carried = carry_state * (jnp.exp(cumulated[-1]) * keep_in[-1])[:, None, None]
        new_state = carried + jnp.einsum(
            "jh,jn,jhp->hnp", to_end, block_b, block_vals, precision=PRECISE
        )
        return (new_state, intra_out + inter_out)

    init_state = jnp.zeros((heads_n, state_n, head_size), values.dtype)
    inputs = (
        blocked(values),
        blocked(log_decay),
        blocked(steps_dt),
        blocked(b_mat),
        blocked(c_mat),
        blocked(segment),
        prev_lasts,
    )
    scan_out = lax.scan(one_block, init_state, inputs)[1]
    return scan_out.reshape(row_count, heads_n, head_size)


def mixer_core(
    zx_rows,
    dt_raw,
    b_conv,
    c_conv,
    conv_wx,
    conv_bx,
    a_log,
    dt_bias,
    d_skip,
    segment=None,
    heads_n=1,
):
    inner_n = zx_rows.shape[1] // 2
    row_count = zx_rows.shape[0]
    x_conv = jax.nn.silu(causal_conv(zx_rows[:, inner_n:], conv_wx, conv_bx, segment))
    steps_dt = jax.nn.softplus(dt_raw + dt_bias[None, :])
    decay_rate = -jnp.exp(a_log)
    values = x_conv.reshape(row_count, heads_n, inner_n // heads_n)
    mixed_out = (
        ssd_scan(values, steps_dt, decay_rate, b_conv, c_conv, segment, SCAN_BLOCK)
        + d_skip[None, :, None] * values
    )
    return mixed_out.reshape(row_count, inner_n) * jax.nn.silu(zx_rows[:, :inner_n])


def bc_core(bc_pre, conv_wbc, conv_bbc, segment=None):
    return jax.nn.silu(causal_conv(bc_pre, conv_wbc, conv_bbc, segment))


def per_device(
    tokens,
    cotangent,
    seq_lens,
    input_norm_gain,
    w_zx,
    w_bc,
    w_dt,
    conv_wx,
    conv_bx,
    conv_wbc,
    conv_bbc,
    a_log,
    dt_bias,
    d_skip,
    norm_gate,
    w_out,
):
    x_full, cot_full = (
        lax.all_gather(tokens, "tensor", axis=1, tiled=True),
        lax.all_gather(cotangent, "tensor", axis=1, tiled=True),
    )
    row_count = tokens.shape[0]
    feat_n = tokens.shape[1]
    feat_start = lax.axis_index("tensor") * feat_n
    state_n = w_bc.shape[1] // 2
    inner_loc = norm_gate.shape[0]
    segment = segment_ids(seq_lens[0], row_count)
    is_live = (segment < seq_lens.shape[1])[:, None]
    w_zx_flat = w_zx.reshape(D, 2 * inner_loc)
    tok_float = x_full.astype(jnp.float32)
    inverse_root_mean = lax.rsqrt(jnp.mean(tok_float * tok_float, axis=1, keepdims=True) + NORM_EPS)
    unit_scaled_input = tok_float * inverse_root_mean
    normed = (unit_scaled_input * input_norm_gain[None, :]).astype(jnp.bfloat16)
    zx_rows = jnp.dot(normed, w_zx_flat, preferred_element_type=jnp.float32)
    bc_pre = jnp.dot(normed, w_bc, preferred_element_type=jnp.float32)
    dt_raw = jnp.dot(normed, w_dt, preferred_element_type=jnp.float32)
    bc_post, bc_back = jax.vjp(partial(bc_core, segment=segment), bc_pre, conv_wbc, conv_bbc)
    gated_rows, core_back = jax.vjp(
        partial(mixer_core, segment=segment, heads_n=a_log.shape[0]),
        zx_rows,
        dt_raw,
        bc_post[:, :state_n],
        bc_post[:, state_n:],
        conv_wx,
        conv_bx,
        a_log,
        dt_bias,
        d_skip,
    )
    cot_live = jnp.where(is_live, cot_full, jnp.zeros_like(cot_full))
    d_gate = contract_cols(cot_live, w_out)
    d_hat = d_gate * norm_gate[None, :]
    squares, cross_sum = lax.psum(
        (
            jnp.sum(gated_rows * gated_rows, axis=1, keepdims=True),
            jnp.sum(d_hat * gated_rows, axis=1, keepdims=True),
        ),
        "tensor",
    )
    r_gate = lax.rsqrt(squares / INNER + NORM_EPS)
    gate_hat = gated_rows * r_gate
    gate_out = (gate_hat * norm_gate[None, :]).astype(jnp.bfloat16)
    branch_part = jnp.dot(gate_out, w_out, preferred_element_type=jnp.float32)
    branch = lax.psum_scatter(branch_part, "tensor", scatter_dimension=1, tiled=True)
    own_float = tokens.astype(jnp.float32)
    block_out = (own_float + jnp.where(is_live, branch, 0.0)).astype(jnp.bfloat16)
    grad_out = contract_rows(gate_out, cot_live)
    grad_gate = jnp.sum(d_gate * gate_hat, axis=0)
    d_gated = r_gate * d_hat - gated_rows * (r_gate * r_gate * r_gate * cross_sum / INNER)
    d_zx, d_dt, d_b, d_c, grad_conv_wx, grad_conv_bx, grad_a_log, grad_dt_bias, grad_d_skip = (
        core_back(d_gated)
    )
    d_bc_post = lax.psum(jnp.concatenate([d_b, d_c], axis=1), "tensor")
    d_bc, grad_conv_wbc, grad_conv_bbc = bc_back(d_bc_post)
    d_zx_half = d_zx.astype(jnp.bfloat16)
    d_bc_half = d_bc.astype(jnp.bfloat16)
    d_dt_half = d_dt.astype(jnp.bfloat16)
    grad_zx = contract_rows(normed, d_zx_half)
    grad_bc = contract_rows(normed, d_bc_half)
    grad_dt = contract_rows(normed, d_dt_half)
    partial_in = contract_cols(d_zx_half, w_zx_flat) + contract_cols(d_dt_half, w_dt)
    own_hat = lax.dynamic_slice_in_dim(unit_scaled_input, feat_start, feat_n, 1)
    own_gain = lax.dynamic_slice_in_dim(input_norm_gain, feat_start, feat_n, 0)
    normed_input_gradient = lax.psum(partial_in, "tensor") + contract_cols(d_bc_half, w_bc)
    unit_input_gradient = normed_input_gradient * input_norm_gain[None, :]
    row_inner_product = jnp.mean(unit_input_gradient * unit_scaled_input, axis=1, keepdims=True)
    own_dn = lax.dynamic_slice_in_dim(normed_input_gradient, feat_start, feat_n, 1)
    own_dxhat = own_dn * own_gain[None, :]
    grad_in = jnp.sum(own_dn * own_hat, axis=0)
    d_tokens = cotangent.astype(jnp.float32) + inverse_root_mean * (
        own_dxhat - own_hat * row_inner_product
    )
    grad_zx_sum, grad_bc_sum, grad_dt_sum, grad_out_sum = (
        lax.psum_scatter(grad_zx, "dp", scatter_dimension=0, tiled=True),
        lax.psum_scatter(grad_bc, "dp", scatter_dimension=0, tiled=True),
        lax.psum_scatter(grad_dt, "dp", scatter_dimension=0, tiled=True),
        lax.psum_scatter(grad_out, "dp", scatter_dimension=1, tiled=True),
    )
    smalls = lax.psum(
        (
            grad_conv_wx,
            grad_conv_bx,
            grad_conv_wbc,
            grad_conv_bbc,
            grad_a_log,
            grad_dt_bias,
            grad_d_skip,
            grad_gate,
            grad_in,
        ),
        "dp",
    )
    grad_zx_out = grad_zx_sum.reshape(grad_zx_sum.shape[0], 2, inner_loc)
    return (
        block_out,
        d_tokens,
        grad_zx_out,
        grad_bc_sum,
        grad_dt_sum,
        grad_out_sum,
        smalls[0],
        smalls[1],
        smalls[2],
        smalls[3],
        smalls[4],
        smalls[5],
        smalls[6],
        smalls[7],
        smalls[8],
    )


def solution(mesh):
    in_specs = (
        P("dp", "tensor"),
        P("dp", "tensor"),
        P("dp", None),
        P(),
        P(None, None, "tensor"),
        P(),
        P(None, "tensor"),
        P(None, "tensor"),
        P("tensor"),
        P(),
        P(),
        P("tensor"),
        P("tensor"),
        P("tensor"),
        P("tensor"),
        P("tensor", None),
    )
    out_specs = (
        P("dp", "tensor"),
        P("dp", "tensor"),
        P("dp", None, "tensor"),
        P("dp", None),
        P("dp", "tensor"),
        P("tensor", "dp"),
        P(None, "tensor"),
        P("tensor"),
        P(),
        P(),
        P("tensor"),
        P("tensor"),
        P("tensor"),
        P("tensor"),
        P("tensor"),
    )
    return jax.shard_map(
        per_device, mesh=mesh, in_specs=in_specs, out_specs=out_specs, check_vma=False
    )
```

profile of v0, /device:TPU:0, one launch (start us, length us, event | category | flops | bytes accessed | tf_op | source)
XLA Modules:
  0.0 829.0 jit_solution(16119154186207128450)
XLA Ops:
  10.0 5.4 copy.202
  16.9 32.0 %all-gather.3.cloned.1.call-done = bf16[512,1536]{1,0:T(8,128)(2,1)} async-done(((bf16[512,384]{1,0:T(8,128)(2,1)}), bf16[512,1536]{1,0:T(8,128)(2,1)}) %all-gather.3.cloned.1.call-update) | async-done | bytes 1572880 | tf_op jit(solution)/shard_map/all_gather | solution.py:149
  50.9 4.6 fusion.165
  58.2 2.9 fusion.137
  61.1 3.0 copy.128
  64.1 3.1 reshape.497
  67.2 3.0 copy.131
  77.3 106.6 %while.83 = (s32[]{:T(128)}, f32[12,128,64]{1,2,0:T(8,128)}, f32[2,256,12,64]{1,0,3,2:T(2,128)}, pred[2,256,256,12]{2,1,3,0:T(32,128)(4,1)}, f32[2,256,256,12]{2...) while((s32[]{:T(128)}, f32[12,128,64]{1,2,0:T(8,128)}, ...), condition=%wide.region_6.7_spmd.clone, body=%wide.region_3.6_spmd.clone.sunk | while | flops 1318172672 | bytes 44319708 | solution.py:96
  89.8 5.1 multiply_dynamic-update-slice_fusion.2
  98.1 3.7 fusion.232
  103.5 16.8 %dynamic_update_slice.292 = f32[2,256,12,64]{1,0,3,2:T(2,128)} dynamic-update-slice(f32[2,256,12,64]{1,0,3,2:T(2,128)} %get-tuple-element.2383, f32[1,256,12,64]{1,0,3,2:T(1,128)} %copy.250, s32[]{:T(128)} %get-tuple-element.2381, s32[]{:T(128)} %constant.210.clone.1..sunk, s32[]{:T(128)} %constant.210.clone.1..sunk, s32[]{:T(128)} %constant.210.clone.1..sunk) | dynamic-update-slice | bytes 1572868 | tf_op jit(solution)/shard_map/jvp()/while/body/jit(dynamic_update_index_in_dim)/dynamic_update_slice | solution.py:96
  142.3 5.1 multiply_dynamic-update-slice_fusion.2
  151.7 3.7 fusion.232
  157.2 16.8 %dynamic_update_slice.292 = f32[2,256,12,64]{1,0,3,2:T(2,128)} dynamic-update-slice(f32[2,256,12,64]{1,0,3,2:T(2,128)} %get-tuple-element.2383, f32[1,256,12,64]{1,0,3,2:T(1,128)} %copy.250, s32[]{:T(128)} %get-tuple-element.2381, s32[]{:T(128)} %constant.210.clone.1..sunk, s32[]{:T(128)} %constant.210.clone.1..sunk, s32[]{:T(128)} %constant.210.clone.1..sunk) | dynamic-update-slice | bytes 1572868 | tf_op jit(solution)/shard_map/jvp()/while/body/jit(dynamic_update_index_in_dim)/dynamic_update_slice | solution.py:96
  186.6 3.0 copy.133
  189.6 4.3 multiply_reduce_fusion.9
  193.9 10.0 %psum.91 = f32[512,1]{0,1:T(1,128)S(1)} all-reduce(f32[512,1]{0,1:T(1,128)S(1)} %bitcast.544), channel_id=1, replica_groups=mesh['dp'=8,'tensor'=4] {'tensor'}, use_global_device_ids=true, to_apply=%region_8.9 | all-reduce | flops 512 | bytes 4096 | tf_op jit(solution)/shard_map/psum | solution.py:183
  204.0 5.1 multiply_reduce_fusion.2
  209.1 8.7 %psum.92 = f32[512,1]{0,1:T(1,128)S(1)} all-reduce(f32[512,1]{0,1:T(1,128)S(1)} %bitcast.550), channel_id=1, replica_groups=mesh['dp'=8,'tensor'=4] {'tensor'}, use_global_device_ids=true, to_apply=%region_11.12 | all-reduce | flops 512 | bytes 4096 | tf_op jit(solution)/shard_map/psum | solution.py:183
  217.8 5.8 multiply_reduce_fusion.3
  223.6 3.1 copy.134
  226.7 3.1 reshape.501
  234.2 146.2 %while.84 = (s32[]{:T(128)}, f32[12,128,64]{1,2,0:T(8,128)S(1)}, f32[2,256,12,64]{1,0,3,2:T(2,128)}, f32[2,256,12]{1,0,2:T(2,128)}, f32[2,256,12]{1,0,2:T(2,128)...) while((s32[]{:T(128)}, f32[12,128,64]{1,2,0:T(8,128)S(1)}, ...), condition=%wide.region_22.23_spmd.clone, body=%wide.region_12.22_spmd.clone.sunk | while | flops 2628679680 | bytes 40395960 | solution.py:96
  238.0 7.7 fusion.249
  245.7 2.9 fusion.247
  262.9 3.2 reduce-window.59
  271.0 4.1 fusion.248
  276.8 16.8 %dynamic_update_slice.296 = f32[2,256,12,64]{1,0,3,2:T(2,128)} dynamic-update-slice(f32[2,256,12,64]{1,0,3,2:T(2,128)} %get-tuple-element.2486, f32[1,256,12,64]{1,0,3,2:T(1,128)} %copy.256, s32[]{:T(128)S(6)} %sub.239, s32[]{:T(128)} %constant.210.clone.1..sunk.1, s32[]{:T(128)} %constant.210.clone.1..sunk.1, s32[]{:T(128)} %constant.210.clone.1..sunk.1) | dynamic-update-slice | bytes 1572868 | tf_op jit(solution)/shard_map/transpose(jvp())/while/body/jit(dynamic_update_index_in_dim)/dynamic_update_slice | solution.py:96
  310.8 7.7 fusion.249
  318.5 2.9 fusion.247
  335.8 3.2 reduce-window.59
  343.8 4.1 fusion.248
  349.7 16.8 %dynamic_update_slice.296 = f32[2,256,12,64]{1,0,3,2:T(2,128)} dynamic-update-slice(f32[2,256,12,64]{1,0,3,2:T(2,128)} %get-tuple-element.2486, f32[1,256,12,64]{1,0,3,2:T(1,128)} %copy.256, s32[]{:T(128)S(6)} %sub.239, s32[]{:T(128)} %constant.210.clone.1..sunk.1, s32[]{:T(128)} %constant.210.clone.1..sunk.1, s32[]{:T(128)} %constant.210.clone.1..sunk.1) | dynamic-update-slice | bytes 1572868 | tf_op jit(solution)/shard_map/transpose(jvp())/while/body/jit(dynamic_update_index_in_dim)/dynamic_update_slice | solution.py:96
  384.6 3.1 copy.139
  387.8 3.9 multiply_reduce_fusion.7
  404.8 3.0 fusion.150
  408.0 4.9 fusion.162
  412.9 8.7 %fusion.145 = f32[1536,1536]{1,0:T(8,128)} fusion(f32[512,768]{1,0:T(8,128)} %copy-done.19, f32[512,768]{1,0:T(8,128)} %get-tuple-element.1867, f32[1536]{0:T(1024)S(1)} %copy-done.67, f32[512]{0:T(512)S(1)} %copy-done.64, bf16[512,1536]{1,0:T(8,128)(2,1)} %all-gather.3.cloned.1.call-done), kind=kOutput, calls=%fused_computation.248 | convolution fusion | flops 2420637696 | bytes 14163968 | tf_op jit(solution)/shard_map/dot_general | solution.py:15
  421.9 119.7 %all-reduce.30.cloned.1.call-done = (f32[512,1536]{1,0:T(8,128)}, f32[512,256]{1,0:T(8,128)}) async-done(((f32[512,1536]{1,0:T(8,128)}, f32[512,256]{1,0:T(8,128)}), (f32[512,1536]{1,0:T(8,128)}, f32[512,256]{1,0:T(8,128)})) %all-reduce.30.cloned.1.call-update) | async-done | bytes 3670032 | tf_op jit(solution)/shard_map/psum | solution.py:214
  548.3 5.7 fusion.139
  554.9 24.2 %reduce-scatter.16.cloned.1.call-done = f32[192,12]{1,0:T(8,128)} async-done(((f32[1536,12]{1,0:T(8,128)}), f32[192,12]{1,0:T(8,128)}) %reduce-scatter.16.cloned.1.call-update) | async-done | bytes 9232
  580.8 3.6 multiply_reduce_fusion.1
  585.6 23.7 %all-reduce.26 = (f32[4,768]{1,0:T(4,128)}, f32[768]{0:T(1024)}, f32[4,256]{1,0:T(4,128)}, f32[256]{0:T(256)}, f32[12]{0:T(128)}, /*index=5*/f32[12]{0:T(128)}, f32[12]{0:T(128)}, f32[768]{0:T(1024)}, f32[384]{0:T(512)}) all-reduce(f32[4,768]{1,0:T(4,128)S(1)} %pad_add_fusion, ...), channel_id=1, replica_groups=mesh['dp'=8,'tensor'=4] {'dp'}, use_global_device_ids=true, to_apply=%region_34.35 | all-reduce | flops 6308 | bytes 50464 | tf_op jit(solution)/shard_map/psum | solution.py:229
  609.3 32.4 %reduce-scatter.8.cloned.1.call-done = f32[512,384]{1,0:T(8,128)} async-done(((f32[512,1536]{1,0:T(8,128)}), f32[512,384]{1,0:T(8,128)}) %reduce-scatter.8.cloned.1.call-update) | async-done | bytes 786448 | tf_op jit(solution)/shard_map/reduce_scatter | solution.py:194
  643.8 78.0 %reduce-scatter.10.cloned.1.call-done = f32[192,1536]{1,0:T(8,128)} async-done(((f32[1536,1536]{1,0:T(8,128)}), f32[192,1536]{1,0:T(8,128)}) %reduce-scatter.10.cloned.1.call-update) | async-done | bytes 1179664 | tf_op jit(solution)/shard_map/reduce_scatter | solution.py:224
  721.9 3.0 reshape.507
  724.8 39.3 %reduce-scatter.12.cloned.1.call-done = f32[192,256]{1,0:T(8,128)} async-done(((f32[1536,256]{1,0:T(8,128)}), f32[192,256]{1,0:T(8,128)}) %reduce-scatter.12.cloned.1.call-update) | async-done | bytes 196624 | tf_op jit(solution)/shard_map/reduce_scatter | solution.py:225
  764.1 57.9 %reduce-scatter.14.cloned.1.call-done = f32[768,192]{0,1:T(8,128)} async-done(((f32[768,1536]{0,1:T(8,128)}), f32[768,192]{0,1:T(8,128)}) %reduce-scatter.14.cloned.1.call-update) | async-done | bytes 589840 | tf_op jit(solution)/shard_map/reduce_scatter | solution.py:227
  (479 shorter events, 183.4 us)
Async XLA Ops:
  7.2 196.8 %copy-start = (bf16[768,1536]{1,0:T(8,128)(2,1)S(1)}, bf16[768,1536]{1,0:T(8,128)(2,1)}, u32[]{:S(2)}) copy-start(bf16[768,1536]{1,0:T(8,128)(2,1)} %param.35) | copy-start | bytes 7077892
  7.2 41.7 %all-gather.3.cloned.1.call-start = ((), (), s32[]{:S(2)}) async-start(), calls=%async_computation.5 | async-start | bytes 1966080 | tf_op jit(solution)/shard_map/all_gather | solution.py:149
  7.9 196.0 %all-gather.5.cloned.1.call-start = ((), (), s32[]{:S(2)}) async-start(), calls=%async_computation.7 | async-start | bytes 1966080 | tf_op jit(solution)/shard_map/all_gather | solution.py:150
  8.7 533.0 %all-reduce.30.cloned.1.call-start = ((), (), s32[]{:S(2)}) async-start(), calls=%async_computation.12 | async-start | bytes 7340032 | tf_op jit(solution)/shard_map/psum | solution.py:214
  9.9 5.5 copy-start.69
  9.9 5.5 copy-start.82
  9.9 5.6 copy-start.88
  9.9 5.6 copy-start.86
  15.4 35.5 %copy-start.66 = (f32[1536]{0:T(1024)S(1)}, f32[1536]{0:T(1024)}, u32[]{:S(2)}) copy-start(f32[1536]{0:T(1024)} %param.23) | copy-start | bytes 18436
  15.4 40.4 %copy-start.52 = (f32[768]{0:T(1024)}, f32[768]{0:T(1024)S(1)}, u32[]{:S(2)}) copy-start(f32[768]{0:T(1024)S(1)} %get-tuple-element.1672) | copy-start | bytes 9220
  15.5 40.4 %copy-start.54 = (f32[768]{0:T(1024)}, f32[768]{0:T(1024)S(1)}, u32[]{:S(2)}) copy-start(f32[768]{0:T(1024)S(1)} %get-tuple-element.1674) | copy-start | bytes 9220
  15.5 40.4 %copy-start.56 = (f32[768]{0:T(1024)}, f32[768]{0:T(1024)S(1)}, u32[]{:S(2)}) copy-start(f32[768]{0:T(1024)S(1)} %get-tuple-element.1673) | copy-start | bytes 9220
  15.5 40.4 %copy-start.58 = (f32[768]{0:T(1024)}, f32[768]{0:T(1024)S(1)}, u32[]{:S(2)}) copy-start(f32[768]{0:T(1024)S(1)} %get-tuple-element.1675) | copy-start | bytes 9220
  15.5 55.3 %copy-start.70 = (f32[1,256]{1,0:T(1,128)}, f32[1,256]{1,0:T(1,128)S(1)}, u32[]{:S(2)}) copy-start(f32[1,256]{1,0:T(1,128)S(1)} %get-tuple-element.1883) | copy-start | bytes 3076
  15.5 55.3 %copy-start.72 = (f32[1,256]{1,0:T(1,128)}, f32[1,256]{1,0:T(1,128)S(1)}, u32[]{:S(2)}) copy-start(f32[1,256]{1,0:T(1,128)S(1)} %get-tuple-element.1885) | copy-start | bytes 3076
  15.5 55.3 %copy-start.74 = (f32[1,256]{1,0:T(1,128)}, f32[1,256]{1,0:T(1,128)S(1)}, u32[]{:S(2)}) copy-start(f32[1,256]{1,0:T(1,128)S(1)} %get-tuple-element.1884) | copy-start | bytes 3076
  15.5 55.3 %copy-start.76 = (f32[1,256]{1,0:T(1,128)}, f32[1,256]{1,0:T(1,128)S(1)}, u32[]{:S(2)}) copy-start(f32[1,256]{1,0:T(1,128)S(1)} %get-tuple-element.1886) | copy-start | bytes 3076
  15.6 57.4 %copy-start.84 = (f32[12]{0:T(128)}, f32[12]{0:T(128)S(1)}, u32[]{:S(2)}) copy-start(f32[12]{0:T(128)S(1)} %exponential_negate_fusion) | copy-start | bytes 148
  15.7 202.1 %copy-start.38 = (f32[768]{0:T(1024)}, f32[768]{0:T(1024)S(1)}, u32[]{:S(2)}) copy-start(f32[768]{0:T(1024)S(1)} %mul.1008) | copy-start | bytes 9220
  16.9 54.0 %copy-start.42 = (f32[512]{0:T(512)}, f32[512]{0:T(512)S(1)}, u32[]{:S(2)}) copy-start(f32[512]{0:T(512)S(1)} %get-tuple-element.1888) | copy-start | bytes 6148
  16.9 54.0 %copy-start.44 = (f32[512]{0:T(512)}, f32[512]{0:T(512)S(1)}, u32[]{:S(2)}) copy-start(f32[512]{0:T(512)S(1)} %get-tuple-element.1889) | copy-start | bytes 6148
  16.9 54.0 %copy-start.46 = (f32[512]{0:T(512)}, f32[512]{0:T(512)S(1)}, u32[]{:S(2)}) copy-start(f32[512]{0:T(512)S(1)} %get-tuple-element.1890) | copy-start | bytes 6148
  50.9 22.2 %copy-start.63 = (f32[512]{0:T(512)}, f32[512]{0:T(512)S(1)}, u32[]{:S(2)}) copy-start(f32[512]{0:T(512)S(1)} %add_rsqrt_fusion.1) | copy-start | bytes 6148
  55.9 5.3 copy-start.13
  77.4 7.4 copy-start.50
  86.2 8.7 %copy-start.40 = (f32[12]{0:T(128)}, f32[12]{0:T(128)S(1)}, u32[]{:S(2)}) copy-start(f32[12]{0:T(128)S(1)} %get-tuple-element.2281) | copy-start | bytes 148 | tf_op jit(solution)/shard_map/jvp()/while
  123.1 5.7 copy-start.32
  123.1 7.0 copy-start.51
  130.1 7.3 copy-start.50
  138.7 8.7 %copy-start.40 = (f32[12]{0:T(128)}, f32[12]{0:T(128)S(1)}, u32[]{:S(2)}) copy-start(f32[12]{0:T(128)S(1)} %get-tuple-element.2281) | copy-start | bytes 148 | tf_op jit(solution)/shard_map/jvp()/while
  176.8 5.7 copy-start.32
  176.8 7.0 copy-start.51
  189.6 14.4 %copy-start.35 = (f32[768]{0:T(1024)S(1)}, f32[768]{0:T(1024)}, u32[]{:S(2)}) copy-start(f32[768]{0:T(1024)} %param.34) | copy-start | bytes 9220
  189.6 14.4 %copy-start.78 = (pred[512]{0:T(512)(128)(4,1)S(1)}, pred[512]{0:T(512)(128)(4,1)}, u32[]{:S(2)}) copy-start(pred[512]{0:T(512)(128)(4,1)} %get-tuple-element.1887) | copy-start | bytes 1540
  204.0 13.9 %copy-start.60 = (f32[512,1]{0,1:T(1,128)}, f32[512,1]{0,1:T(1,128)S(1)}, u32[]{:S(2)}) copy-start(f32[512,1]{0,1:T(1,128)S(1)} %add_rsqrt_fusion) | copy-start | bytes 6148
  293.6 5.2 copy-start.18
  300.8 4.8 copy-start.92
  366.4 5.2 copy-start.18
  373.6 4.8 copy-start.92
  396.4 5.3 copy-start.19
  404.2 175.0 %reduce-scatter.16.cloned.1.call-start = ((), (), s32[]{:S(2)}) async-start(), calls=%async_computation.11 | async-start | bytes 884736
  407.9 233.9 %reduce-scatter.8.cloned.1.call-start = ((), (), s32[]{:S(2)}) async-start(), calls=%async_computation.6 | async-start | bytes 3932160 | tf_op jit(solution)/shard_map/reduce_scatter | solution.py:194
  412.9 309.0 %reduce-scatter.10.cloned.1.call-start = ((), (), s32[]{:S(2)}) async-start(), calls=%async_computation.8 | async-start | bytes 10616832 | tf_op jit(solution)/shard_map/reduce_scatter | solution.py:224
  421.7 120.0 %copy-start.8 = (f32[512,256]{1,0:T(8,128)S(1)}, f32[512,256]{1,0:T(8,128)}, u32[]{:S(2)}) copy-start(f32[512,256]{1,0:T(8,128)} %copy-done.7) | copy-start | bytes 1572868
  421.7 120.0 %copy-start.17 = (f32[512,256]{1,0:T(8,128)S(1)}, f32[512,256]{1,0:T(8,128)}, u32[]{:S(2)}) copy-start(f32[512,256]{1,0:T(8,128)} %get-tuple-element.1843) | copy-start | bytes 1572868
  421.7 342.4 %reduce-scatter.12.cloned.1.call-start = ((), (), s32[]{:S(2)}) async-start(), calls=%async_computation.9 | async-start | bytes 1769472 | tf_op jit(solution)/shard_map/reduce_scatter | solution.py:225
  547.7 274.3 %reduce-scatter.14.cloned.1.call-start = ((), (), s32[]{:S(2)}) async-start(), calls=%async_computation.10 | async-start | bytes 5308416 | tf_op jit(solution)/shard_map/reduce_scatter | solution.py:227
  584.4 57.4 %copy-start.21 = (bf16[512,384]{1,0:T(8,128)(2,1)S(1)}, bf16[512,384]{1,0:T(8,128)(2,1)}, u32[]{:S(2)}) copy-start(bf16[512,384]{1,0:T(8,128)(2,1)} %param.20) | copy-start | bytes 1179652
  (78 other events, 188.9 us)
Sparse Core Ops, SparseCore 0:
  9.6 39.3 all-gather.2
  50.5 35.9 all-gather.4
  404.3 137.2 all-reduce.29
  545.2 33.9 reduce-scatter.15
  581.3 60.4 reduce-scatter.7
  645.1 76.6 reduce-scatter.9
  725.7 38.3 reduce-scatter.11
  768.1 53.7 reduce-scatter.13
where the time goes:
time: 843 us; the launch traced here: 829 us
  waiting for transfers between devices  385 us (46%)
  local copies, waits for them, and re-layouts  178 us (21%)
  matrix products  116 us (14%)
  other arithmetic  90.7 us (11%)
  blocking collectives  42.4 us (5%)
  between operations  15.3 us (2%)
    psum x1, waiting for transfers between devices, per_device(): lax.psum(partial_in, 'tensor') + contract_cols(d_bc_half, w_bc)  120 us
    dynamic_update_slice x26, local copies, waits for them, and re-layouts, ssd_scan(): scan_out = lax.scan(one_block, init_state, inputs)[1]  87.3 us
    reduce_scatter x1, waiting for transfers between devices, per_device(): lax.psum_scatter(grad_zx, 'dp', scatter_dimension=0, tiled=True)  78 us
    reduce_scatter x1, waiting for transfers between devices, per_device(): lax.psum_scatter(grad_out, 'dp', scatter_dimension=1, tiled=True)  57.9 us
    reduce_scatter x1, waiting for transfers between devices, per_device(): lax.psum_scatter(grad_bc, 'dp', scatter_dimension=0, tiled=True)  39.3 us
    reduce_scatter x1, waiting for transfers between devices, per_device(): lax.psum_scatter(branch_part, 'tensor', scatter_dimension=1, tiled=True)  32.4 us
    all_gather x1, waiting for transfers between devices, per_device(): lax.all_gather(tokens, 'tensor', axis=1, tiled=True)  32 us
    dot_general x6, matrix products, one_block(): jnp.einsum('ijh,jhp->ihp', mixing, block_vals, precision=PRECISE)  31.2 us
  transfers between devices with their start and end apart: 8, of which 7 were waited for; matrix products, arithmetic and copies ran while one was open for 22% of the time, Pallas kernels for 0%

commit v1 on v0

--- a/solution.py
+++ b/solution.py
@@ -211,7 +211,9 @@
     partial_in = contract_cols(d_zx_half, w_zx_flat) + contract_cols(d_dt_half, w_dt)
     own_hat = lax.dynamic_slice_in_dim(unit_scaled_input, feat_start, feat_n, 1)
     own_gain = lax.dynamic_slice_in_dim(input_norm_gain, feat_start, feat_n, 0)
-    normed_input_gradient = lax.psum(partial_in, "tensor") + contract_cols(d_bc_half, w_bc)
+    normed_input_gradient = jnp.sum(lax.all_gather(partial_in, "tensor"), axis=0) + contract_cols(
+        d_bc_half, w_bc
+    )
     unit_input_gradient = normed_input_gradient * input_norm_gain[None, :]
     row_inner_product = jnp.mean(unit_input_gradient * unit_scaled_input, axis=1, keepdims=True)
     own_dn = lax.dynamic_slice_in_dim(normed_input_gradient, feat_start, feat_n, 1)

time: 843 us -> 940 us (1.12)
  waiting for transfers between devices: 385 us -> 472 us
  other arithmetic: 90.7 us -> 103 us
    all_gather x0 -> x1, waiting for transfers between devices: none -> 217 us  [per_device(): lax.all_gather(partial_in, 'tensor')]
    psum x1, waiting for transfers between devices: 120 us -> 0.02 us  [per_device(): d_bc_post = lax.psum(jnp.concatenate([d_b, d_c], axis=1), 'tensor')]
    reduce_scatter x1, waiting for transfers between devices: 39.3 us -> 2.67 us  [per_device(): lax.psum_scatter(grad_bc, 'dp', scatter_dimension=0, tiled=True)]
    reduce_scatter x1, waiting for transfers between devices: 32.4 us -> 61 us  [per_device(): lax.psum_scatter(branch_part, 'tensor', scatter_dimension=1, tiled=True)]
    unnamed x154 -> x170, local copies, waits for them, and re-layouts: 28.6 us -> 26.2 us
    unnamed x9 -> x10, waiting for transfers between devices: 25.7 us -> 24 us
  transfers between devices with their start and end apart: 8 -> 9, of which waited for: 7 -> 7; matrix products, arithmetic and copies ran while one was open for 22% -> 23% of each run, Pallas kernels for 0% -> 0%
where the time goes in v1:
time: 940 us; the launch traced here: 927 us
  waiting for transfers between devices  472 us (50%)
  local copies, waits for them, and re-layouts  175 us (19%)
  matrix products  115 us (12%)
  other arithmetic  103 us (11%)
  blocking collectives  43.5 us (5%)
  between operations  15.2 us (2%)
    all_gather x1, waiting for transfers between devices, per_device(): lax.all_gather(partial_in, 'tensor')  217 us
    dynamic_update_slice x26, local copies, waits for them, and re-layouts, ssd_scan(): scan_out = lax.scan(one_block, init_state, inputs)[1]  87.3 us
    reduce_scatter x1, waiting for transfers between devices, per_device(): lax.psum_scatter(grad_zx, 'dp', scatter_dimension=0, tiled=True)  78.1 us
    reduce_scatter x1, waiting for transfers between devices, per_device(): lax.psum_scatter(branch_part, 'tensor', scatter_dimension=1, tiled=True)  61 us
    reduce_scatter x1, waiting for transfers between devices, per_device(): lax.psum_scatter(grad_out, 'dp', scatter_dimension=1, tiled=True)  57.8 us
    all_gather x1, waiting for transfers between devices, per_device(): lax.all_gather(tokens, 'tensor', axis=1, tiled=True)  32.1 us
    dot_general x6, matrix products, one_block(): jnp.einsum('ijh,jhp->ihp', mixing, block_vals, precision=PRECISE)  31.2 us
    dynamic_update_slice x14, other arithmetic, ssd_scan(): scan_out = lax.scan(one_block, init_state, inputs)[1]  27.6 us
  transfers between devices with their start and end apart: 9, of which 7 were waited for; matrix products, arithmetic and copies ran while one was open for 23% of the time, Pallas kernels for 0%

profile of v1, /device:TPU:0, one launch (start us, length us, event | category | flops | bytes accessed | tf_op | source)
XLA Modules:
  0.0 926.6 jit_solution(12249426394314015088)
XLA Ops:
  10.0 5.5 copy.203
  16.9 32.1 %all-gather.5.cloned.1.call-done = bf16[512,1536]{1,0:T(8,128)(2,1)} async-done(((bf16[512,384]{1,0:T(8,128)(2,1)}), bf16[512,1536]{1,0:T(8,128)(2,1)}) %all-gather.5.cloned.1.call-update) | async-done | bytes 1572880 | tf_op jit(solution)/shard_map/all_gather | solution.py:149
  50.9 4.6 fusion.165
  58.2 2.9 fusion.137
  61.1 3.0 copy.128
  64.2 3.1 reshape.497
  67.2 2.9 copy.131
  77.3 106.7 %while.83 = (s32[]{:T(128)}, f32[12,128,64]{1,2,0:T(8,128)}, f32[2,256,12,64]{1,0,3,2:T(2,128)}, pred[2,256,256,12]{2,1,3,0:T(32,128)(4,1)}, f32[2,256,256,12]{2...) while((s32[]{:T(128)}, f32[12,128,64]{1,2,0:T(8,128)}, ...), condition=%wide.region_6.7_spmd.clone, body=%wide.region_3.6_spmd.clone.sunk | while | flops 1318172672 | bytes 44319708 | solution.py:96
  89.8 5.1 multiply_dynamic-update-slice_fusion.2
  98.1 3.7 fusion.232
  103.6 16.8 %dynamic_update_slice.292 = f32[2,256,12,64]{1,0,3,2:T(2,128)} dynamic-update-slice(f32[2,256,12,64]{1,0,3,2:T(2,128)} %get-tuple-element.2381, f32[1,256,12,64]{1,0,3,2:T(1,128)} %copy.251, s32[]{:T(128)} %get-tuple-element.2379, s32[]{:T(128)} %constant.210.clone.1..sunk, s32[]{:T(128)} %constant.210.clone.1..sunk, s32[]{:T(128)} %constant.210.clone.1..sunk) | dynamic-update-slice | bytes 1572868 | tf_op jit(solution)/shard_map/jvp()/while/body/jit(dynamic_update_index_in_dim)/dynamic_update_slice | solution.py:96
  142.5 5.1 multiply_dynamic-update-slice_fusion.2
  151.9 3.7 fusion.232
  157.3 16.8 %dynamic_update_slice.292 = f32[2,256,12,64]{1,0,3,2:T(2,128)} dynamic-update-slice(f32[2,256,12,64]{1,0,3,2:T(2,128)} %get-tuple-element.2381, f32[1,256,12,64]{1,0,3,2:T(1,128)} %copy.251, s32[]{:T(128)} %get-tuple-element.2379, s32[]{:T(128)} %constant.210.clone.1..sunk, s32[]{:T(128)} %constant.210.clone.1..sunk, s32[]{:T(128)} %constant.210.clone.1..sunk) | dynamic-update-slice | bytes 1572868 | tf_op jit(solution)/shard_map/jvp()/while/body/jit(dynamic_update_index_in_dim)/dynamic_update_slice | solution.py:96
  186.7 3.0 copy.133
  189.7 4.4 multiply_reduce_fusion.9
  194.1 10.0 %psum.84 = f32[512,1]{0,1:T(1,128)S(1)} all-reduce(f32[512,1]{0,1:T(1,128)S(1)} %bitcast.544), channel_id=1, replica_groups=mesh['dp'=8,'tensor'=4] {'tensor'}, use_global_device_ids=true, to_apply=%region_8.9 | all-reduce | flops 512 | bytes 4096 | tf_op jit(solution)/shard_map/psum | solution.py:183
  204.2 5.1 multiply_reduce_fusion.2
  209.4 8.6 psum.85
  218.0 5.8 multiply_reduce_fusion.3
  223.8 3.1 copy.134
  226.9 3.1 reshape.501
  234.4 146.2 %while.84 = (s32[]{:T(128)}, f32[12,128,64]{1,2,0:T(8,128)S(1)}, f32[2,256,12,64]{1,0,3,2:T(2,128)}, f32[2,256,12]{1,0,2:T(2,128)}, f32[2,256,12]{1,0,2:T(2,128)...) while((s32[]{:T(128)}, f32[12,128,64]{1,2,0:T(8,128)S(1)}, ...), condition=%wide.region_22.23_spmd.clone, body=%wide.region_12.22_spmd.clone.sunk | while | flops 2628679680 | bytes 40395960 | solution.py:96
  238.2 7.7 fusion.249
  263.1 3.2 reduce-window.59
  271.2 4.1 fusion.248
  277.0 16.8 %dynamic_update_slice.296 = f32[2,256,12,64]{1,0,3,2:T(2,128)} dynamic-update-slice(f32[2,256,12,64]{1,0,3,2:T(2,128)} %get-tuple-element.2484, f32[1,256,12,64]{1,0,3,2:T(1,128)} %copy.257, s32[]{:T(128)S(6)} %sub.239, s32[]{:T(128)} %constant.210.clone.1..sunk.1, s32[]{:T(128)} %constant.210.clone.1..sunk.1, s32[]{:T(128)} %constant.210.clone.1..sunk.1) | dynamic-update-slice | bytes 1572868 | tf_op jit(solution)/shard_map/transpose(jvp())/while/body/jit(dynamic_update_index_in_dim)/dynamic_update_slice | solution.py:96
  311.0 7.7 fusion.249
  318.7 2.9 fusion.247
  335.9 3.2 reduce-window.59
  344.0 4.1 fusion.248
  349.8 16.8 %dynamic_update_slice.296 = f32[2,256,12,64]{1,0,3,2:T(2,128)} dynamic-update-slice(f32[2,256,12,64]{1,0,3,2:T(2,128)} %get-tuple-element.2484, f32[1,256,12,64]{1,0,3,2:T(1,128)} %copy.257, s32[]{:T(128)S(6)} %sub.239, s32[]{:T(128)} %constant.210.clone.1..sunk.1, s32[]{:T(128)} %constant.210.clone.1..sunk.1, s32[]{:T(128)} %constant.210.clone.1..sunk.1) | dynamic-update-slice | bytes 1572868 | tf_op jit(solution)/shard_map/transpose(jvp())/while/body/jit(dynamic_update_index_in_dim)/dynamic_update_slice | solution.py:96
  383.4 3.1 fusion.150
  386.6 4.5 fusion.162
  393.9 3.0 copy.139
  396.9 3.9 multiply_reduce_fusion.7
  407.8 5.4 fusion.145
  413.3 5.5 fusion.146
  429.7 5.7 fusion.139
  436.4 22.5 %reduce-scatter.16.cloned.1.call-done = f32[192,12]{1,0:T(8,128)} async-done(((f32[1536,12]{1,0:T(8,128)}), f32[192,12]{1,0:T(8,128)}) %reduce-scatter.16.cloned.1.call-update) | async-done | bytes 9232
  460.5 61.0 %reduce-scatter.8.cloned.1.call-done = f32[512,384]{1,0:T(8,128)} async-done(((f32[512,1536]{1,0:T(8,128)}), f32[512,384]{1,0:T(8,128)}) %reduce-scatter.8.cloned.1.call-update) | async-done | bytes 786448 | tf_op jit(solution)/shard_map/reduce_scatter | solution.py:194
  523.6 78.1 %reduce-scatter.10.cloned.1.call-done = f32[192,1536]{1,0:T(8,128)} async-done(((f32[1536,1536]{1,0:T(8,128)}), f32[192,1536]{1,0:T(8,128)}) %reduce-scatter.10.cloned.1.call-update) | async-done | bytes 1179664 | tf_op jit(solution)/shard_map/reduce_scatter | solution.py:226
  601.6 3.0 reshape.507
  604.6 216.8 %all-gather.9.cloned.1.call-done = f32[2048,1536]{1,0:T(8,128)} async-done(((f32[512,1536]{1,0:T(8,128)}), f32[2048,1536]{1,0:T(8,128)}) %all-gather.9.cloned.1.call-update) | async-done | bytes 12582928 | tf_op jit(solution)/shard_map/all_gather | solution.py:214
  821.4 8.0 reduce_sum.392
  829.4 3.8 multiply_reduce_fusion.1
  834.5 24.9 %all-reduce.26 = (f32[4,768]{1,0:T(4,128)}, f32[768]{0:T(1024)}, f32[4,256]{1,0:T(4,128)}, f32[256]{0:T(256)}, f32[12]{0:T(128)}, /*index=5*/f32[12]{0:T(128)}, f32[12]{0:T(128)}, f32[768]{0:T(1024)}, f32[384]{0:T(512)}) all-reduce(f32[4,768]{1,0:T(4,128)S(1)} %pad_add_fusion, ...), channel_id=1, replica_groups=mesh['dp'=8,'tensor'=4] {'dp'}, use_global_device_ids=true, to_apply=%region_34.35 | all-reduce | flops 6308 | bytes 50464 | tf_op jit(solution)/shard_map/psum | solution.py:231
  862.0 57.8 %reduce-scatter.14.cloned.1.call-done = f32[768,192]{0,1:T(8,128)} async-done(((f32[768,1536]{0,1:T(8,128)}), f32[768,192]{0,1:T(8,128)}) %reduce-scatter.14.cloned.1.call-update) | async-done | bytes 589840 | tf_op jit(solution)/shard_map/reduce_scatter | solution.py:229
  (498 shorter events, 188.1 us)
Async XLA Ops:
  7.2 197.0 %copy-start = (bf16[768,1536]{1,0:T(8,128)(2,1)S(1)}, bf16[768,1536]{1,0:T(8,128)(2,1)}, u32[]{:S(2)}) copy-start(bf16[768,1536]{1,0:T(8,128)(2,1)} %param.35) | copy-start | bytes 7077892
  7.2 41.7 %all-gather.5.cloned.1.call-start = ((), (), s32[]{:S(2)}) async-start(), calls=%async_computation.5 | async-start | bytes 1966080 | tf_op jit(solution)/shard_map/all_gather | solution.py:149
  7.9 196.3 %all-gather.7.cloned.1.call-start = ((), (), s32[]{:S(2)}) async-start(), calls=%async_computation.7 | async-start | bytes 1966080 | tf_op jit(solution)/shard_map/all_gather | solution.py:150
  8.7 412.5 %all-reduce.29.cloned.1.call-start = ((), (), s32[]{:S(2)}) async-start(), calls=%async_computation.8 | async-start | bytes 1048576 | tf_op jit(solution)/shard_map/psum | solution.py:203
  9.9 5.5 copy-start.72
  9.9 5.6 copy-start.90
  9.9 5.6 copy-start.98
  9.9 5.7 copy-start.96
  15.4 35.4 %copy-start.68 = (f32[1536]{0:T(1024)S(1)}, f32[1536]{0:T(1024)}, u32[]{:S(2)}) copy-start(f32[1536]{0:T(1024)} %param.23) | copy-start | bytes 18436
  15.5 40.4 %copy-start.52 = (f32[768]{0:T(1024)}, f32[768]{0:T(1024)S(1)}, u32[]{:S(2)}) copy-start(f32[768]{0:T(1024)S(1)} %get-tuple-element.1672) | copy-start | bytes 9220
  15.5 40.4 %copy-start.54 = (f32[768]{0:T(1024)}, f32[768]{0:T(1024)S(1)}, u32[]{:S(2)}) copy-start(f32[768]{0:T(1024)S(1)} %get-tuple-element.1674) | copy-start | bytes 9220
  15.5 40.4 %copy-start.56 = (f32[768]{0:T(1024)}, f32[768]{0:T(1024)S(1)}, u32[]{:S(2)}) copy-start(f32[768]{0:T(1024)S(1)} %get-tuple-element.1673) | copy-start | bytes 9220
  15.5 40.4 %copy-start.58 = (f32[768]{0:T(1024)}, f32[768]{0:T(1024)S(1)}, u32[]{:S(2)}) copy-start(f32[768]{0:T(1024)S(1)} %get-tuple-element.1675) | copy-start | bytes 9220
  15.5 55.3 %copy-start.73 = (f32[1,256]{1,0:T(1,128)}, f32[1,256]{1,0:T(1,128)S(1)}, u32[]{:S(2)}) copy-start(f32[1,256]{1,0:T(1,128)S(1)} %get-tuple-element.1881) | copy-start | bytes 3076
  15.6 55.3 %copy-start.75 = (f32[1,256]{1,0:T(1,128)}, f32[1,256]{1,0:T(1,128)S(1)}, u32[]{:S(2)}) copy-start(f32[1,256]{1,0:T(1,128)S(1)} %get-tuple-element.1883) | copy-start | bytes 3076
  15.6 55.3 %copy-start.77 = (f32[1,256]{1,0:T(1,128)}, f32[1,256]{1,0:T(1,128)S(1)}, u32[]{:S(2)}) copy-start(f32[1,256]{1,0:T(1,128)S(1)} %get-tuple-element.1882) | copy-start | bytes 3076
  15.6 55.3 %copy-start.79 = (f32[1,256]{1,0:T(1,128)}, f32[1,256]{1,0:T(1,128)S(1)}, u32[]{:S(2)}) copy-start(f32[1,256]{1,0:T(1,128)S(1)} %get-tuple-element.1884) | copy-start | bytes 3076
  15.6 57.4 %copy-start.93 = (f32[12]{0:T(128)}, f32[12]{0:T(128)S(1)}, u32[]{:S(2)}) copy-start(f32[12]{0:T(128)S(1)} %exponential_negate_fusion) | copy-start | bytes 148
  15.8 202.3 %copy-start.38 = (f32[768]{0:T(1024)}, f32[768]{0:T(1024)S(1)}, u32[]{:S(2)}) copy-start(f32[768]{0:T(1024)S(1)} %mul.1008) | copy-start | bytes 9220
  16.9 54.0 %copy-start.42 = (f32[512]{0:T(512)}, f32[512]{0:T(512)S(1)}, u32[]{:S(2)}) copy-start(f32[512]{0:T(512)S(1)} %get-tuple-element.1886) | copy-start | bytes 6148
  16.9 54.0 %copy-start.44 = (f32[512]{0:T(512)}, f32[512]{0:T(512)S(1)}, u32[]{:S(2)}) copy-start(f32[512]{0:T(512)S(1)} %get-tuple-element.1887) | copy-start | bytes 6148
  16.9 54.0 %copy-start.46 = (f32[512]{0:T(512)}, f32[512]{0:T(512)S(1)}, u32[]{:S(2)}) copy-start(f32[512]{0:T(512)S(1)} %get-tuple-element.1888) | copy-start | bytes 6148
  50.9 22.2 %copy-start.63 = (f32[512]{0:T(512)}, f32[512]{0:T(512)S(1)}, u32[]{:S(2)}) copy-start(f32[512]{0:T(512)S(1)} %add_rsqrt_fusion.1) | copy-start | bytes 6148
  55.9 5.3 copy-start.13
  77.5 7.4 copy-start.50
  86.2 8.7 copy-start.40
  123.2 5.7 copy-start.30
  123.2 7.0 copy-start.51
  130.2 7.4 copy-start.50
  138.9 8.7 copy-start.40
  176.9 5.7 copy-start.30
  177.0 7.0 copy-start.51
  189.7 14.5 %copy-start.33 = (f32[768]{0:T(1024)S(1)}, f32[768]{0:T(1024)}, u32[]{:S(2)}) copy-start(f32[768]{0:T(1024)} %param.34) | copy-start | bytes 9220
  189.7 14.5 %copy-start.81 = (pred[512]{0:T(512)(128)(4,1)S(1)}, pred[512]{0:T(512)(128)(4,1)}, u32[]{:S(2)}) copy-start(pred[512]{0:T(512)(128)(4,1)} %get-tuple-element.1885) | copy-start | bytes 1540
  204.2 13.9 %copy-start.60 = (f32[512,1]{0,1:T(1,128)}, f32[512,1]{0,1:T(1,128)S(1)}, u32[]{:S(2)}) copy-start(f32[512,1]{0,1:T(1,128)S(1)} %add_rsqrt_fusion) | copy-start | bytes 6148
  366.6 5.2 copy-start.18
  382.5 76.4 %reduce-scatter.16.cloned.1.call-start = ((), (), s32[]{:S(2)}) async-start(), calls=%async_computation.13 | async-start | bytes 884736
  386.5 135.0 %reduce-scatter.8.cloned.1.call-start = ((), (), s32[]{:S(2)}) async-start(), calls=%async_computation.6 | async-start | bytes 3932160 | tf_op jit(solution)/shard_map/reduce_scatter | solution.py:194
  391.1 210.5 %reduce-scatter.10.cloned.1.call-start = ((), (), s32[]{:S(2)}) async-start(), calls=%async_computation.9 | async-start | bytes 10616832 | tf_op jit(solution)/shard_map/reduce_scatter | solution.py:226
  413.2 5.6 copy-start.49
  413.2 408.2 %all-gather.9.cloned.1.call-start = ((), (), s32[]{:S(2)}) async-start(), calls=%async_computation.12 | async-start | bytes 15728640 | tf_op jit(solution)/shard_map/all_gather | solution.py:214
  421.1 440.9 %reduce-scatter.12.cloned.1.call-start = ((), (), s32[]{:S(2)}) async-start(), calls=%async_computation.10 | async-start | bytes 1769472 | tf_op jit(solution)/shard_map/reduce_scatter | solution.py:227
  429.1 490.7 %reduce-scatter.14.cloned.1.call-start = ((), (), s32[]{:S(2)}) async-start(), calls=%async_computation.11 | async-start | bytes 5308416 | tf_op jit(solution)/shard_map/reduce_scatter | solution.py:229
  435.4 25.1 %copy-start.85 = (f32[256]{0:T(256)S(1)}, f32[256]{0:T(256)}, u32[]{:S(2)}) copy-start(f32[256]{0:T(256)} %get-tuple-element.1824) | copy-start | bytes 3076
  435.4 25.1 %copy-start.86 = (f32[256]{0:T(256)S(1)}, f32[256]{0:T(256)}, u32[]{:S(2)}) copy-start(f32[256]{0:T(256)} %get-tuple-element.1827) | copy-start | bytes 3076
  435.4 25.1 %copy-start.87 = (f32[256]{0:T(256)S(1)}, f32[256]{0:T(256)}, u32[]{:S(2)}) copy-start(f32[256]{0:T(256)} %get-tuple-element.1874) | copy-start | bytes 3076
  435.4 25.1 %copy-start.88 = (f32[256]{0:T(256)S(1)}, f32[256]{0:T(256)}, u32[]{:S(2)}) copy-start(f32[256]{0:T(256)} %get-tuple-element.1671) | copy-start | bytes 3076
  435.4 86.1 %copy-start.21 = (bf16[512,384]{1,0:T(8,128)(2,1)S(1)}, bf16[512,384]{1,0:T(8,128)(2,1)}, u32[]{:S(2)}) copy-start(bf16[512,384]{1,0:T(8,128)(2,1)} %param.20) | copy-start | bytes 1179652
  (87 other events, 208.6 us)
Sparse Core Ops, SparseCore 0:
  9.6 39.3 all-gather.4
  50.5 35.9 all-gather.6
  382.7 37.8 all-reduce.28
  424.1 34.7 reduce-scatter.15
  461.1 60.3 reduce-scatter.7
  524.9 76.7 reduce-scatter.9
  603.2 218.1 all-gather.8
  825.3 36.6 reduce-scatter.11
  866.0 53.7 reduce-scatter.13
